TPU v7x, 8 devices: a whole 2x2x1 slice. The times are simulated.
8 devices in a mesh: dp: 1 (over z), tp: 2 (over y), sp: 4 (over x, core).
Axes of the slice: x: 2, y: 2, z: 1, core: 2. Of those that a mesh axis runs over, the one named last changes fastest.
Arguments:
- x_tokens: bfloat16 [2048, 4096], P(('dp', 'sp'), 'tp')
- doc_ids: int32 [2048], P(('dp', 'sp'))
- w_qkv: bfloat16 [4096, 12288], P('sp', 'tp')
- w_out: bfloat16 [4096, 4096], P('sp', 'tp')
Outputs:
- output: bfloat16 [2048, 4096], P(('dp', 'sp', 'tp'))
All inputs are finite; a program needn't handle non-finite values.
Results may differ from a plain program's by a relative error of at most 0.00248.
Values are sent between devices in bfloat16 or wider.
A program may use at most 1 GiB of HBM per device.

v0:
```python
import jax
import jax.numpy as jnp
from jax import lax
from jax.sharding import PartitionSpec as P

HEAD_DIM = 128
SOFTMAX_SCALE = HEAD_DIM ** -0.5


def solution(mesh):
    def device_block(x_block, doc_block, wqkv_block, wout_block):
        x_rows = lax.all_gather(x_block, "tp", axis=1, tiled=True)
        wqkv_cols = lax.all_gather(wqkv_block, "sp", axis=0, tiled=True)
        qkv_local = jnp.dot(x_rows, wqkv_cols, preferred_element_type=jnp.float32).astype(jnp.bfloat16)
        row_count = x_rows.shape[0]
        head_count = wqkv_cols.shape[1] // (3 * HEAD_DIM)
        qkv_local = qkv_local.reshape(row_count, head_count, 3, HEAD_DIM)
        query_loc = qkv_local[:, :, 0]
        kv_all = lax.all_gather(qkv_local[:, :, 1:], "sp", axis=0, tiled=True)
        doc_all = lax.all_gather(doc_block, "sp", axis=0, tiled=True)
        scores = jnp.einsum("qhd,khd->hqk", query_loc, kv_all[:, :, 0], preferred_element_type=jnp.float32) * SOFTMAX_SCALE
        same_doc = doc_block[:, None] == doc_all[None, :]
        scores = jnp.where(same_doc[None], scores, -jnp.inf)
        weights = jax.nn.softmax(scores, axis=-1).astype(jnp.bfloat16)
        context = jnp.einsum("hqk,khd->qhd", weights, kv_all[:, :, 1], preferred_element_type=jnp.float32).astype(jnp.bfloat16)
        context = context.reshape(row_count, head_count * HEAD_DIM)
        ctx_rows = lax.all_gather(context, "tp", axis=1, tiled=True)
        wout_cols = lax.all_gather(wout_block, "sp", axis=0, tiled=True)
        y_block = jnp.dot(ctx_rows, wout_cols, preferred_element_type=jnp.float32).astype(jnp.bfloat16)
        return lax.all_to_all(y_block, "tp", 0, 1, tiled=True)

    return jax.shard_map(
        device_block,
        mesh=mesh,
        in_specs=(P(("dp", "sp"), "tp"), P(("dp", "sp")), P("sp", "tp"), P("sp", "tp")),
        out_specs=P(("dp", "sp", "tp"), None),
        check_vma=False,
    )
```

profile of v0, /device:TPU:0, one launch (start us, length us, event | category | flops | bytes accessed | tf_op | source)
XLA Modules:
  0.0 745.8 jit_solution(7216485107075675194)
XLA Ops:
  6.5 0.0 all-gather.7.cloned.1.call-start
  6.5 0.7 all-gather.7.cloned.1.call-update
  7.3 0.0 all-gather.9.cloned.1.call-start
  7.3 0.7 all-gather.9.cloned.1.call-update
  8.0 0.0 all-gather.11.cloned.1.call-start
  8.1 57.8 %all-gather.7.cloned.1.call-done = bf16[512,4096]{1,0:T(8,128)(2,1)} async-done(((bf16[512,2048]{1,0:T(8,128)(2,1)}), bf16[512,4096]{1,0:T(8,128)(2,1)}) %all-gather.7.cloned.1.call-update) | async-done | bytes 4194320 | tf_op jit(solution)/shard_map/all_gather | solution.py:12
  65.9 296.1 %all-gather.9.cloned.1.call-done = bf16[4096,6144]{1,0:T(8,128)(2,1)} async-done(((bf16[1024,6144]{1,0:T(8,128)(2,1)}), bf16[4096,6144]{1,0:T(8,128)(2,1)}) %all-gather.9.cloned.1.call-update) | async-done | bytes 50331664 | tf_op jit(solution)/shard_map/all_gather | solution.py:13
  362.0 33.7 %convolution_convert_fusion = bf16[512,6144]{1,0:T(8,128)(2,1)} fusion(bf16[512,4096]{1,0:T(8,128)(2,1)} %all-gather.7.cloned.1.call-done, bf16[4096,6144]{1,0:T(8,128)(2,1)} %all-gather.9.cloned.1.call-done), kind=kOutput, calls=%fused_computation.9 | convolution fusion | flops 25772949504 | bytes 60817408 | tf_op jit(solution)/shard_map/dot_general | solution.py:14
  395.6 0.0 copy-start
  395.6 8.6 %copy.14 = bf16[512,6144]{0,1:T(8,128)(2,1)} copy(bf16[512,6144]{1,0:T(8,128)(2,1)} %convolution_convert_fusion) | data formatting | bytes 12582912 | tf_op jit(solution)/shard_map/convert_element_type | solution.py:14
  404.3 4.6 slice.16
  408.9 6.2 copy.20
  415.1 0.0 all-gather.11.cloned.1.call-update
  415.1 0.0 all-gather.15.cloned.1.call-start
  415.1 0.5 all-gather.15.cloned.1.call-update
  415.7 0.0 all-gather.13.cloned.1.call-start
  415.7 0.0 copy-done
  415.7 7.0 all-gather
  422.7 0.7 broadcast_compare_fusion
  423.4 96.0 %all-gather.11.cloned.1.call-done = bf16[2048,16,2,128]{3,0,1,2:T(8,128)(2,1)} async-done(((bf16[512,16,2,128]{3,0,1,2:T(8,128)(2,1)}), bf16[2048,16,2,128]{3,0,1,2:T(8,128)(2,1)}) %all-gather.11.cloned.1.call-update) | async-done | bytes 16777232 | tf_op jit(solution)/shard_map/all_gather | solution.py:19
  519.4 27.1 %fusion.6 = f32[16,512,2048]{2,1,0:T(8,128)} fusion(bf16[2048,16,2,128]{3,0,1,2:T(8,128)(2,1)} %all-gather.11.cloned.1.call-done, bf16[512,16,3,128]{0,3,2,1:T(8,128)(2,1)} %bitcast.27), kind=kOutput, calls=%fused_computation.11 | convolution fusion | flops 4294967296 | bytes 77594624 | tf_op jit(solution)/shard_map/qhd,khd->hqk/dot_general | solution.py:21
  546.5 68.7 %fusion.10 = (f32[16,512]{1,0:T(8,128)S(1)}, f32[16,512,2048]{2,1,0:T(8,128)}) fusion(f32[16,512,2048]{2,1,0:T(8,128)} %fusion.6, pred[512,2048]{1,0:T(8,128)(4,1)S(1)} %broadcast_compare_fusion), kind=kOutput, calls=%fused_computation.19 | output fusion | flops 100665344 | bytes 135299072 | tf_op jit(solution)/shard_map/sub | solution.py:24
  615.1 27.2 %fusion.7 = bf16[16,128,512]{2,1,0:T(8,128)(2,1)} fusion(f32[16,512,2048]{2,1,0:T(8,128)} %get-tuple-element.6, f32[16,512]{1,0:T(8,128)S(1)} %get-tuple-element.5, bf16[2048,16,2,128]{3,0,1,2:T(8,128)(2,1)} %all-gather.11.cloned.1.call-done), kind=kOutput, calls=%fused_computation.16 | convolution fusion | flops 4329570304 | bytes 77627392 | tf_op jit(solution)/shard_map/hqk,khd->qhd/dot_general | solution.py:25
  642.4 0.0 all-gather.13.cloned.1.call-update
  642.4 0.0 all-gather.15.cloned.1.call-done
  642.4 54.3 %all-gather.13.cloned.1.call-done = bf16[512,4096]{0,1:T(8,128)(2,1)} async-done(((bf16[512,2048]{0,1:T(8,128)(2,1)}), bf16[512,4096]{0,1:T(8,128)(2,1)}) %all-gather.13.cloned.1.call-update) | async-done | bytes 4194320 | tf_op jit(solution)/shard_map/all_gather | solution.py:27
  696.8 13.6 %convolution_convert_fusion.1 = bf16[512,2048]{1,0:T(8,128)(2,1)S(1)} fusion(bf16[512,4096]{0,1:T(8,128)(2,1)} %all-gather.13.cloned.1.call-done, bf16[4096,2048]{1,0:T(8,128)(2,1)} %all-gather.15.cloned.1.call-done), kind=kOutput, calls=%fused_computation.13 | convolution fusion | flops 8590983168 | bytes 23068672 | tf_op jit(solution)/shard_map/dot_general | solution.py:29
  710.4 27.4 %all_to_all.19 = bf16[2,256,2048]{2,1,0:T(8,128)(2,1)S(1)} all-to-all(bf16[2,256,2048]{2,1,0:T(8,128)(2,1)S(1)} %bitcast.30), channel_id=1, replica_groups=mesh['dp'=1,'tp'=2,'sp'=4] {'tp'}, dimensions={0} | all-to-all | bytes 4194304 | tf_op jit(solution)/shard_map/all_to_all | solution.py:30
  737.8 1.5 copy.22
Async XLA Ops:
  6.5 59.4 %all-gather.7.cloned.1.call-start = ((), (), s32[]{:S(2)}) async-start(), calls=%async_computation.1 | async-start | bytes 6291456 | tf_op jit(solution)/shard_map/all_gather | solution.py:12
  7.3 354.7 %all-gather.9.cloned.1.call-start = ((), (), s32[]{:S(2)}) async-start(), calls=%async_computation.2 | async-start | bytes 62914560 | tf_op jit(solution)/shard_map/all_gather | solution.py:13
  8.0 511.4 %all-gather.11.cloned.1.call-start = ((), (), s32[]{:S(2)}) async-start(), calls=%async_computation.3 | async-start | bytes 20971520 | tf_op jit(solution)/shard_map/all_gather | solution.py:19
  395.6 20.1 %copy-start = (s32[512]{0:T(512)S(1)}, s32[512]{0:T(512)}, u32[]{:S(2)}) copy-start(s32[512]{0:T(512)} %param.5) | copy-start | bytes 6148
  415.1 227.4 %all-gather.15.cloned.1.call-start = ((), (), s32[]{:S(2)}) async-start(), calls=%async_computation.5 | async-start | bytes 20971520 | tf_op jit(solution)/shard_map/all_gather | solution.py:28
  415.7 281.1 %all-gather.13.cloned.1.call-start = ((), (), s32[]{:S(2)}) async-start(), calls=%async_computation.4 | async-start | bytes 6291456 | tf_op jit(solution)/shard_map/all_gather | solution.py:27
Sparse Core Ops, SparseCore 0:
  8.8 57.0 all-gather.6
  67.4 294.4 all-gather.8
  415.2 104.1 all-gather.10
  520.8 104.1 all-gather.14
  642.5 54.1 all-gather.12
where the time goes:
time: 746 us
  waiting for transfers between devices  506 us (68%)
  matrix products  102 us (14%)
  other arithmetic  69.3 us (9%)
  blocking collectives  34.4 us (5%)
  local copies, waits for them, and re-layouts  20.9 us (3%)
  between operations  13.2 us (2%)
    all_gather x1, waiting for transfers between devices, device_block(): wqkv_cols = lax.all_gather(wqkv_block, 'sp', axis=0, tiled=True)  296 us
    all_gather x1, waiting for transfers between devices, device_block(): kv_all = lax.all_gather(qkv_local[:, :, 1:], 'sp', axis=0, tiled=True)  96 us
    sub x1, other arithmetic, device_block(): weights = jax.nn.softmax(scores, axis=-1).astype(jnp.bfloat16)  68.7 us
    all_gather x1, waiting for transfers between devices, device_block(): x_rows = lax.all_gather(x_block, 'tp', axis=1, tiled=True)  57.8 us
    all_gather x1, waiting for transfers between devices, device_block(): ctx_rows = lax.all_gather(context, 'tp', axis=1, tiled=True)  54.3 us
    dot_general x1, matrix products, device_block(): jnp.dot(x_rows, wqkv_cols, preferred_element_type=jnp.float32)  33.7 us
    all_to_all x1, blocking collectives, device_block(): return lax.all_to_all(y_block, 'tp', 0, 1, tiled=True)  27.4 us
    dot_general x1, matrix products, device_block(): jnp.einsum('hqk,khd->qhd', weights, kv_all[:, :, 1], preferred_element_ty...  27.2 us
  transfers between devices with their start and end apart: 5, of which 4 were waited for; matrix products, arithmetic and copies ran while one was open for 17% of the time, Pallas kernels for 0%

commit v1 on v0

v1 whole, which is shorter than its diff:
```python
import functools

import jax
import jax.numpy as jnp
from jax import lax
from jax.experimental import pallas as pl
from jax.experimental.pallas import tpu as pltpu
from jax.sharding import PartitionSpec as P

HEAD_DIM = 128
SOFTMAX_SCALE = HEAD_DIM ** -0.5
TRIPLE = 3 * HEAD_DIM
SP = 4
TP = 2


def block_kernel(
    x_ref, doc_ref, wqkv_ref, wout_ref, y_ref,
    x_all, w_all, wo_all, o_all, o_own, qkv, y_buf, doc_all, doc_col,
    local_sem, w_local_sem, x_send, x_recv, doc_send, doc_recv, w_send, w_recv,
    wo_local_sem, wo_send, wo_recv, o_send, o_recv, of_send, of_recv, y_send, y_recv, y_local_sem,
):
    me = lax.axis_index("sp")
    col = lax.axis_index("tp")
    rows, half = x_ref.shape
    depth = wqkv_ref.shape[0]
    heads = w_all.shape[0]
    chunks = y_buf.shape[0]
    width = y_buf.shape[2]
    other_col = 1 - col
    chip = me // 2
    core = lax.rem(me, 2)
    mate = chip * 2 + 1 - core
    across = (1 - chip) * 2 + core
    diagonal = (1 - chip) * 2 + 1 - core
    peers = (mate, across, diagonal)

    barrier = pltpu.get_barrier_semaphore()
    for peer in peers:
        pl.semaphore_signal(barrier, inc=1, device_id={"sp": peer}, device_id_type=pl.DeviceIdType.MESH)
    pl.semaphore_signal(barrier, inc=1, device_id={"tp": other_col}, device_id_type=pl.DeviceIdType.MESH)
    pl.semaphore_wait(barrier, 4)

    def remote(src, dst, send, recv, where):
        return pltpu.make_async_remote_copy(
            src_ref=src, dst_ref=dst, send_sem=send, recv_sem=recv,
            device_id=where, device_id_type=pl.DeviceIdType.MESH,
        )

    def x_slot(c, s):
        return x_all.at[c, pl.ds(pl.multiple_of(s * rows, rows), rows), :]

    def x_copy(i, c, s, where, src=None):
        slot = x_slot(c, s)
        return remote(slot if src is None else src, slot, x_send.at[i], x_recv.at[i], where)

    to_mate, to_across, to_col = {"sp": mate}, {"sp": across}, {"tp": other_col}

    x_sends = [
        x_copy(0, col, me, to_mate, x_ref),
        x_copy(1, col, me, to_across, x_ref),
        x_copy(2, col, me, to_col, x_ref),
    ]
    for copy in x_sends:
        copy.start()
    x_local = pltpu.make_async_copy(x_ref, x_slot(col, me), local_sem.at[0])
    x_local.start()
    doc_local = pltpu.make_async_copy(doc_ref, doc_all.at[me], local_sem.at[1])
    doc_local.start()
    doc_sends = []
    for i, peer in enumerate(peers):
        copy = remote(doc_ref, doc_all.at[me], doc_send.at[i], doc_recv.at[i], {"sp": peer})
        copy.start()
        doc_sends.append(copy)

    def w_cols(owner, h):
        start = pl.multiple_of((owner * heads + h) * TRIPLE, TRIPLE)
        return wqkv_ref.at[:, pl.ds(start, TRIPLE)]

    def w_slot(h, s):
        return w_all.at[h, pl.ds(pl.multiple_of(s * depth, depth), depth), :]

    def w_copy(i, h):
        return remote(w_cols(peers[i], h), w_slot(h, me), w_send.at[h, i], w_recv.at[h, i], {"sp": peers[i]})

    def w_local(h):
        return pltpu.make_async_copy(w_cols(me, h), w_slot(h, me), w_local_sem.at[h])

    for h in range(heads):
        w_copy(1, h).start()
        w_copy(2, h).start()
        w_copy(0, h).start()
        w_local(h).start()

    def wo_cols(j):
        return pl.ds(pl.multiple_of(j * width, width), width)

    def wo_slot(s, j):
        return wo_all.at[pl.ds(pl.multiple_of(s * depth, depth), depth), wo_cols(j)]

    wo_local = pltpu.make_async_copy(wout_ref, wo_all.at[pl.ds(pl.multiple_of(me * depth, depth), depth), :], wo_local_sem)
    wo_local.start()

    x_copy(2, other_col, me, to_col).wait_recv()
    x_sends.append(x_copy(5, other_col, me, to_mate))
    x_sends[-1].start()
    x_copy(1, col, across, to_across).wait_recv()
    x_sends.append(x_copy(4, col, across, to_col))
    x_sends[-1].start()
    x_sends.append(x_copy(3, col, across, to_mate))
    x_sends[-1].start()

    doc_local.wait()
    for i, peer in enumerate(peers):
        remote(doc_ref, doc_all.at[peer], doc_send.at[i], doc_recv.at[i], {"sp": peer}).wait_recv()
    for s in range(SP):
        tall = jnp.broadcast_to(doc_all[s], (HEAD_DIM, rows))
        doc_col[pl.ds(s * rows, rows), :] = tall.T

    x_copy(4, other_col, across, to_col).wait_recv()
    x_sends.append(x_copy(6, other_col, across, to_mate))
    x_sends[-1].start()
    x_local.wait()
    x_copy(0, col, mate, to_mate).wait_recv()
    x_copy(3, col, diagonal, to_mate).wait_recv()
    x_copy(5, other_col, mate, to_mate).wait_recv()
    x_copy(6, other_col, diagonal, to_mate).wait_recv()

    def wo_to_mate(j):
        return remote(wout_ref.at[:, wo_cols(j)], wo_slot(me, j), wo_send.at[0, j], wo_recv.at[0, j], to_mate)

    def wo_to_across(j):
        return remote(wout_ref.at[:, wo_cols(j)], wo_slot(me, j), wo_send.at[1, j], wo_recv.at[1, j], to_across)

    def wo_pass(j):
        slot = wo_slot(across, j)
        return remote(slot, slot, wo_send.at[2, j], wo_recv.at[2, j], to_mate)

    def o_slot(c, s, h):
        return o_all.at[c, s, :, pl.ds(pl.multiple_of(h * HEAD_DIM, HEAD_DIM), HEAD_DIM)]

    def o_copy(i, h):
        src = o_own.at[h, pl.ds(pl.multiple_of(peers[i] * rows, rows), rows), :]
        return remote(src, o_slot(col, me, h), o_send.at[h, i], o_recv.at[h, i], {"sp": peers[i]})

    def o_pass(h):
        slot = o_all.at[col, :, :, pl.ds(pl.multiple_of(h * HEAD_DIM, HEAD_DIM), HEAD_DIM)]
        return remote(slot, slot, of_send.at[h], of_recv.at[h], to_col)

    def o_collect(h):
        for i in range(3):
            remote(o_slot(col, peers[i], h), o_slot(col, peers[i], h), o_send.at[h, i], o_recv.at[h, i], {"sp": peers[i]}).wait_recv()
        o_pass(h).start()

    early = chunks // 2

    def one_head(h, carry):
        w_local(h).wait()
        for i in range(3):
            remote(w_cols(peers[i], h), w_slot(h, peers[i]), w_send.at[h, i], w_recv.at[h, i], {"sp": peers[i]}).wait_recv()

        @pl.when(h == heads - 2)
        def _():
            for j in range(early):
                wo_to_across(j).start()

        def project(r, carry):
            tile = pl.ds(pl.multiple_of(r * rows, rows), rows)
            total = jnp.dot(x_all[0, tile, :], w_all[h, :half, :], preferred_element_type=jnp.float32)
            total += jnp.dot(x_all[1, tile, :], w_all[h, half:, :], preferred_element_type=jnp.float32)
            qkv[tile, :] = total.astype(jnp.bfloat16)
            return carry

        lax.fori_loop(0, SP, project, 0)

        docs = jnp.concatenate([doc_all[s] for s in range(SP)], axis=1)

        def attend(r, carry):
            tile = pl.ds(pl.multiple_of(r * 256, 256), 256)
            query = qkv[tile, :HEAD_DIM]
            scores = lax.dot_general(
                query, qkv[:, HEAD_DIM:2 * HEAD_DIM], (((1,), (1,)), ((), ())),
                preferred_element_type=jnp.float32,
            ) * SOFTMAX_SCALE
            same = doc_col[tile, :1] == docs
            scores = jnp.where(same, scores, -jnp.inf)
            top = jnp.max(scores, axis=1, keepdims=True)
            weights = jnp.exp(scores - top)
            weights = weights * (1.0 / jnp.sum(weights, axis=1, keepdims=True))
            out = jnp.dot(weights.astype(jnp.bfloat16), qkv[:, 2 * HEAD_DIM:], preferred_element_type=jnp.float32)
            o_own[h, tile, :] = out.astype(jnp.bfloat16)
            return carry

        lax.fori_loop(0, SP * rows // 256, attend, 0)
        mine = pl.ds(pl.multiple_of(me * rows, rows), rows)
        o_all[col, me, :, pl.ds(pl.multiple_of(h * HEAD_DIM, HEAD_DIM), HEAD_DIM)] = o_own[h, mine, :]
        for i in (1, 2, 0):
            o_copy(i, h).start()

        @pl.when(h >= 1)
        def _():
            o_collect(h - 1)

        return carry

    lax.fori_loop(0, heads, one_head, 0)
    for j in range(early, chunks):
        wo_to_across(j).start()
    for j in range(chunks):
        wo_to_mate(j).start()
    wo_local.wait()
    o_collect(heads - 1)

    def other_half(h):
        slot = o_all.at[other_col, :, :, pl.ds(pl.multiple_of(h * HEAD_DIM, HEAD_DIM), HEAD_DIM)]
        return remote(slot, slot, of_send.at[h], of_recv.at[h], to_col)

    keep = pl.ds(pl.multiple_of(col * (rows // 2), rows // 2), rows // 2)
    give = pl.ds(pl.multiple_of(other_col * (rows // 2), rows // 2), rows // 2)

    def y_cols(c, j):
        return pl.ds(pl.multiple_of(c * (chunks * width) + j * width, width), width)

    def y_copy(j):
        return remote(y_buf.at[j, give, :], y_ref.at[:, y_cols(col, j)], y_send.at[j], y_recv.at[j], to_col)

    def y_local(j):
        return pltpu.make_async_copy(y_buf.at[j, keep, :], y_ref.at[:, y_cols(col, j)], y_local_sem.at[j])

    def y_arrive(j):
        return remote(y_buf.at[j, give, :], y_ref.at[:, y_cols(other_col, j)], y_send.at[j], y_recv.at[j], to_col)

    def pass_on(j):
        slot = wo_slot(across, j)
        remote(slot, slot, wo_send.at[1, j], wo_recv.at[1, j], to_across).wait_recv()
        wo_pass(j).start()

    pass_on(0)
    for h in range(heads):
        other_half(h).wait_recv()

    def finish(j, carry):
        @pl.when(j + 1 < chunks)
        def _():
            pass_on(j + 1)

        slot = wo_slot(mate, j)
        remote(slot, slot, wo_send.at[0, j], wo_recv.at[0, j], to_mate).wait_recv()
        slot = wo_slot(diagonal, j)
        remote(slot, slot, wo_send.at[2, j], wo_recv.at[2, j], to_mate).wait_recv()
        total = jnp.zeros((rows, width), jnp.float32)
        for c in range(TP):
            for s in range(SP):
                k = (c * SP + s) * heads * HEAD_DIM
                total += jnp.dot(
                    o_all[c, s], wo_all[k:k + heads * HEAD_DIM, wo_cols(j)],
                    preferred_element_type=jnp.float32,
                )
        y_buf[j] = total.astype(jnp.bfloat16)
        y_copy(j).start()
        y_local(j).start()
        return carry

    lax.fori_loop(0, chunks, finish, 0)

    for j in range(chunks):
        y_arrive(j).wait_recv()
        y_local(j).wait()
        y_copy(j).wait_send()
        wo_to_across(j).wait_send()
        wo_to_mate(j).wait_send()
        wo_pass(j).wait_send()
    for copy in x_sends + doc_sends:
        copy.wait_send()
    for h in range(heads):
        for i in range(3):
            w_copy(i, h).wait_send()
            o_copy(i, h).wait_send()
        o_pass(h).wait_send()


def solution(mesh):
    def device_block(x_block, doc_block, wqkv_block, wout_block):
        rows, half = x_block.shape
        depth = wqkv_block.shape[0]
        heads = wqkv_block.shape[1] // (TRIPLE * SP)
        cols = wout_block.shape[1]
        chunks = 8
        width = cols // chunks
        bf16 = jnp.bfloat16
        dma = pltpu.SemaphoreType.DMA
        return pl.pallas_call(
            block_kernel,
            out_shape=jax.ShapeDtypeStruct((rows // TP, cols * TP), bf16),
            in_specs=[pl.BlockSpec(memory_space=pl.ANY)] * 4,
            out_specs=pl.BlockSpec(memory_space=pl.ANY),
            scratch_shapes=[
                pltpu.VMEM((TP, SP * rows, half), bf16),
                pltpu.VMEM((heads, SP * depth, TRIPLE), bf16),
                pltpu.VMEM((SP * depth, cols), bf16),
                pltpu.VMEM((TP, SP, rows, heads * HEAD_DIM), bf16),
                pltpu.VMEM((heads, SP * rows, HEAD_DIM), bf16),
                pltpu.VMEM((SP * rows, TRIPLE), bf16),
                pltpu.VMEM((chunks, rows, width), bf16),
                pltpu.VMEM((SP, 1, rows), jnp.int32),
                pltpu.VMEM((SP * rows, HEAD_DIM), jnp.int32),
                dma((2,)),
                dma((heads,)),
                dma((7,)),
                dma((7,)),
                dma((3,)),
                dma((3,)),
                dma((heads, 3)),
                dma((heads, 3)),
                dma,
                dma((3, chunks)),
                dma((3, chunks)),
                dma((heads, 3)),
                dma((heads, 3)),
                dma((heads,)),
                dma((heads,)),
                dma((chunks,)),
                dma((chunks,)),
                dma((chunks,)),
            ],
            compiler_params=pltpu.CompilerParams(
                collective_id=0, has_side_effects=True, vmem_limit_bytes=66 * 1024 * 1024 - 2 * 1024 * 1024 - 65536,
            ),
            name="attention_block",
        )(x_block, doc_block.reshape(1, rows), wqkv_block, wout_block)

    return jax.shard_map(
        device_block,
        mesh=mesh,
        in_specs=(P(("dp", "sp"), "tp"), P(("dp", "sp")), P("sp", "tp"), P("sp", "tp")),
        out_specs=P(("dp", "sp", "tp"), None),
        check_vma=False,
    )
```

time: 746 us -> 311 us (0.42)
  waiting for transfers between devices: 506 us -> 0 us
  Pallas kernels: 0 us -> 307 us
  matrix products: 102 us -> 0 us
  other arithmetic: 69.3 us -> 0 us
  blocking collectives: 34.4 us -> 0 us
  local copies, waits for them, and re-layouts: 20.9 us -> 3.13 us
  between operations: 13.2 us -> 0.01 us
    all_gather x5 -> x0, waiting for transfers between devices: 504 us -> none  [the longest x1 296 us: device_block(): wqkv_cols = lax.all_gather(wqkv_block, 'sp', axis=0, tiled=True)]
    pallas_call x0 -> x1, Pallas kernels: none -> 307 us  [device_block(): pl.pallas_call(block_kernel, out_shape=jax.ShapeDtypeStruct((rows // TP,...]
    dot_general x4 -> x0, matrix products: 102 us -> none  [the longest x1 33.7 us: device_block(): jnp.dot(x_rows, wqkv_cols, preferred_element_type=jnp.float32)]
    sub x1 -> x0, other arithmetic: 68.7 us -> none  [device_block(): weights = jax.nn.softmax(scores, axis=-1).astype(jnp.bfloat16)]
    all_to_all x1 -> x0, blocking collectives: 27.4 us -> none  [device_block(): return lax.all_to_all(y_block, 'tp', 0, 1, tiled=True)]
    convert_element_type x1 -> x0, local copies, waits for them, and re-layouts: 8.64 us -> none  [device_block(): jnp.dot(x_rows, wqkv_cols, preferred_element_type=jnp.float32)]
  transfers between devices with their start and end apart: 5 -> 0, of which waited for: 4 -> 0; matrix products, arithmetic and copies ran while one was open for 17% -> 0% of each run, Pallas kernels for 0% -> 0%
where the time goes in v1:
time: 311 us; the launch traced here: 310 us
  Pallas kernels  307 us (99%)
  local copies, waits for them, and re-layouts  3.13 us (1%)
    pallas_call x1, Pallas kernels, device_block(): pl.pallas_call(block_kernel, out_shape=jax.ShapeDtypeStruct((rows // TP,...  307 us

profile of v1, /device:TPU:0, one launch (start us, length us, event | category | flops | bytes accessed | tf_op | source)
XLA Modules:
  0.0 310.4 jit_solution(14986758581648995130)
XLA Ops:
  0.0 307.3 %attention_block.1 = bf16[256,4096]{1,0:T(8,128)(2,1)} custom-call(bf16[512,2048]{1,0:T(8,128)(2,1)} %x_ref.1, s32[1,512]{1,0:T(1,128)} %bitcast.1, bf16[1024,6144]{1,0:T(8,128)(2,1)} %wqkv_ref.1, bf16[1024,2048]{1,0:T(8,128)(2,1)} %wout_ref.1), custom_call_target="tpu_custom_call" | custom-call | tf_op jit(solution)/shard_map/attention_block/pallas_call | solution.py:292
  307.3 3.1 %copy.6 = bf16[256,4096]{1,0:T(8,128)(2,1)} copy(bf16[256,4096]{1,0:T(8,128)(2,1)} %attention_block.1) | data formatting | bytes 4194304

commit v2 on v1

--- a/solution.py
+++ b/solution.py
@@ -12,21 +12,24 @@
 TRIPLE = 3 * HEAD_DIM
 SP = 4
 TP = 2
+WIDTHS = (384, 384, 384, 384, 256, 128, 128)
+EARLY = 2
 
 
 def block_kernel(
     x_ref, doc_ref, wqkv_ref, wout_ref, y_ref,
-    x_all, w_all, wo_all, o_all, o_own, qkv, y_buf, doc_all, doc_col,
+    x_all, w_all, wo_all, o_all, qkv, doc_all,
     local_sem, w_local_sem, x_send, x_recv, doc_send, doc_recv, w_send, w_recv,
-    wo_local_sem, wo_send, wo_recv, o_send, o_recv, of_send, of_recv, y_send, y_recv, y_local_sem,
+    wo_local_sem, wo_send, wo_recv, o_send, o_recv, of_send, of_recv, y_send, y_recv,
 ):
     me = lax.axis_index("sp")
     col = lax.axis_index("tp")
     rows, half = x_ref.shape
     depth = wqkv_ref.shape[0]
     heads = w_all.shape[0]
-    chunks = y_buf.shape[0]
-    width = y_buf.shape[2]
+    chunks = len(WIDTHS)
+    starts = [sum(WIDTHS[:j]) for j in range(chunks)]
+    cols = wout_ref.shape[1]
     other_col = 1 - col
     chip = me // 2
     core = lax.rem(me, 2)
@@ -93,7 +96,7 @@
         w_local(h).start()
 
     def wo_cols(j):
-        return pl.ds(pl.multiple_of(j * width, width), width)
+        return pl.ds(starts[j], WIDTHS[j])
 
     def wo_slot(s, j):
         return wo_all.at[pl.ds(pl.multiple_of(s * depth, depth), depth), wo_cols(j)]
@@ -113,9 +116,6 @@
     doc_local.wait()
     for i, peer in enumerate(peers):
         remote(doc_ref, doc_all.at[peer], doc_send.at[i], doc_recv.at[i], {"sp": peer}).wait_recv()
-    for s in range(SP):
-        tall = jnp.broadcast_to(doc_all[s], (HEAD_DIM, rows))
-        doc_col[pl.ds(s * rows, rows), :] = tall.T
 
     x_copy(4, other_col, across, to_col).wait_recv()
     x_sends.append(x_copy(6, other_col, across, to_mate))
@@ -140,7 +140,7 @@
         return o_all.at[c, s, :, pl.ds(pl.multiple_of(h * HEAD_DIM, HEAD_DIM), HEAD_DIM)]
 
     def o_copy(i, h):
-        src = o_own.at[h, pl.ds(pl.multiple_of(peers[i] * rows, rows), rows), :]
+        src = w_all.at[h, pl.ds(pl.multiple_of(peers[i] * rows, rows), rows), pl.ds(0, HEAD_DIM)]
         return remote(src, o_slot(col, me, h), o_send.at[h, i], o_recv.at[h, i], {"sp": peers[i]})
 
     def o_pass(h):
@@ -152,7 +152,7 @@
             remote(o_slot(col, peers[i], h), o_slot(col, peers[i], h), o_send.at[h, i], o_recv.at[h, i], {"sp": peers[i]}).wait_recv()
         o_pass(h).start()
 
-    early = chunks // 2
+    early = EARLY
 
     def one_head(h, carry):
         w_local(h).wait()
@@ -182,18 +182,19 @@
                 query, qkv[:, HEAD_DIM:2 * HEAD_DIM], (((1,), (1,)), ((), ())),
                 preferred_element_type=jnp.float32,
             ) * SOFTMAX_SCALE
-            same = doc_col[tile, :1] == docs
+            own = doc_all[r // 2, :, pl.ds(pl.multiple_of(lax.rem(r, 2) * 256, 256), 256)]
+            same = jnp.broadcast_to(own, (HEAD_DIM, 256)).T[:, :1] == docs
             scores = jnp.where(same, scores, -jnp.inf)
             top = jnp.max(scores, axis=1, keepdims=True)
             weights = jnp.exp(scores - top)
             weights = weights * (1.0 / jnp.sum(weights, axis=1, keepdims=True))
             out = jnp.dot(weights.astype(jnp.bfloat16), qkv[:, 2 * HEAD_DIM:], preferred_element_type=jnp.float32)
-            o_own[h, tile, :] = out.astype(jnp.bfloat16)
+            w_all[h, tile, :HEAD_DIM] = out.astype(jnp.bfloat16)
             return carry
 
         lax.fori_loop(0, SP * rows // 256, attend, 0)
         mine = pl.ds(pl.multiple_of(me * rows, rows), rows)
-        o_all[col, me, :, pl.ds(pl.multiple_of(h * HEAD_DIM, HEAD_DIM), HEAD_DIM)] = o_own[h, mine, :]
+        o_all[col, me, :, pl.ds(pl.multiple_of(h * HEAD_DIM, HEAD_DIM), HEAD_DIM)] = w_all[h, mine, :HEAD_DIM]
         for i in (1, 2, 0):
             o_copy(i, h).start()
 
@@ -215,57 +216,57 @@
         slot = o_all.at[other_col, :, :, pl.ds(pl.multiple_of(h * HEAD_DIM, HEAD_DIM), HEAD_DIM)]
         return remote(slot, slot, of_send.at[h], of_recv.at[h], to_col)
 
-    keep = pl.ds(pl.multiple_of(col * (rows // 2), rows // 2), rows // 2)
-    give = pl.ds(pl.multiple_of(other_col * (rows // 2), rows // 2), rows // 2)
+    span = rows // 2
+    keep = pl.ds(pl.multiple_of(col * span, span), span)
+    give = pl.ds(pl.multiple_of(other_col * span, span), span)
 
     def y_cols(c, j):
-        return pl.ds(pl.multiple_of(c * (chunks * width) + j * width, width), width)
+        return pl.ds(pl.multiple_of(c * cols + starts[j], HEAD_DIM), WIDTHS[j])
+
+    def given_slot(j):
+        return w_all.at[heads - 1, pl.ds(SP * rows + j * span, span), pl.ds(0, WIDTHS[j])]
 
     def y_copy(j):
-        return remote(y_buf.at[j, give, :], y_ref.at[:, y_cols(col, j)], y_send.at[j], y_recv.at[j], to_col)
-
-    def y_local(j):
-        return pltpu.make_async_copy(y_buf.at[j, keep, :], y_ref.at[:, y_cols(col, j)], y_local_sem.at[j])
+        return remote(given_slot(j), y_ref.at[:, y_cols(col, j)], y_send.at[j], y_recv.at[j], to_col)
 
     def y_arrive(j):
-        return remote(y_buf.at[j, give, :], y_ref.at[:, y_cols(other_col, j)], y_send.at[j], y_recv.at[j], to_col)
-
-    def pass_on(j):
+        return remote(given_slot(j), y_ref.at[:, y_cols(other_col, j)], y_send.at[j], y_recv.at[j], to_col)
+
+    def part(owner, piece, j):
+        total = None
+        for i in range(2):
+            block = (owner % 2) * 2 + i
+            first = pl.multiple_of(owner * depth + i * (depth // 2), depth // 2)
+            term = jnp.dot(
+                o_all[owner // 2, block, piece, :], wo_all[pl.ds(first, depth // 2), wo_cols(j)],
+                preferred_element_type=jnp.float32,
+            )
+            total = term if total is None else total + term
+        return total
+
+    for h in range(heads):
+        other_half(h).wait_recv()
+
+    for j in range(chunks):
+        slot = wo_slot(mate, j)
+        remote(slot, slot, wo_send.at[0, j], wo_recv.at[0, j], to_mate).wait_recv()
+        given = part(me, give, j) + part(mate, give, j)
+        kept = part(me, keep, j) + part(mate, keep, j)
         slot = wo_slot(across, j)
         remote(slot, slot, wo_send.at[1, j], wo_recv.at[1, j], to_across).wait_recv()
         wo_pass(j).start()
-
-    pass_on(0)
-    for h in range(heads):
-        other_half(h).wait_recv()
-
-    def finish(j, carry):
-        @pl.when(j + 1 < chunks)
-        def _():
-            pass_on(j + 1)
-
-        slot = wo_slot(mate, j)
-        remote(slot, slot, wo_send.at[0, j], wo_recv.at[0, j], to_mate).wait_recv()
+        given += part(across, give, j)
+        kept += part(across, keep, j)
         slot = wo_slot(diagonal, j)
         remote(slot, slot, wo_send.at[2, j], wo_recv.at[2, j], to_mate).wait_recv()
-        total = jnp.zeros((rows, width), jnp.float32)
-        for c in range(TP):
-            for s in range(SP):
-                k = (c * SP + s) * heads * HEAD_DIM
-                total += jnp.dot(
-                    o_all[c, s], wo_all[k:k + heads * HEAD_DIM, wo_cols(j)],
-                    preferred_element_type=jnp.float32,
-                )
-        y_buf[j] = total.astype(jnp.bfloat16)
+        given += part(diagonal, give, j)
+        w_all[heads - 1, pl.ds(SP * rows + j * span, span), :WIDTHS[j]] = given.astype(jnp.bfloat16)
+        kept += part(diagonal, keep, j)
         y_copy(j).start()
-        y_local(j).start()
-        return carry
-
-    lax.fori_loop(0, chunks, finish, 0)
+        y_ref[:, y_cols(col, j)] = kept.astype(jnp.bfloat16)
 
     for j in range(chunks):
         y_arrive(j).wait_recv()
-        y_local(j).wait()
         y_copy(j).wait_send()
         wo_to_across(j).wait_send()
         wo_to_mate(j).wait_send()
@@ -285,25 +286,21 @@
         depth = wqkv_block.shape[0]
         heads = wqkv_block.shape[1] // (TRIPLE * SP)
         cols = wout_block.shape[1]
-        chunks = 8
-        width = cols // chunks
+        chunks = len(WIDTHS)
         bf16 = jnp.bfloat16
         dma = pltpu.SemaphoreType.DMA
         return pl.pallas_call(
             block_kernel,
-            out_shape=jax.ShapeDtypeStruct((rows // TP, cols * TP), bf16),
+            out_shape=pltpu.VMEM((rows // TP, cols * TP), bf16),
             in_specs=[pl.BlockSpec(memory_space=pl.ANY)] * 4,
-            out_specs=pl.BlockSpec(memory_space=pl.ANY),
+            out_specs=pl.BlockSpec(memory_space=pltpu.VMEM),
             scratch_shapes=[
                 pltpu.VMEM((TP, SP * rows, half), bf16),
                 pltpu.VMEM((heads, SP * depth, TRIPLE), bf16),
                 pltpu.VMEM((SP * depth, cols), bf16),
                 pltpu.VMEM((TP, SP, rows, heads * HEAD_DIM), bf16),
-                pltpu.VMEM((heads, SP * rows, HEAD_DIM), bf16),
                 pltpu.VMEM((SP * rows, TRIPLE), bf16),
-                pltpu.VMEM((chunks, rows, width), bf16),
                 pltpu.VMEM((SP, 1, rows), jnp.int32),
-                pltpu.VMEM((SP * rows, HEAD_DIM), jnp.int32),
                 dma((2,)),
                 dma((heads,)),
                 dma((7,)),
@@ -321,10 +318,9 @@
                 dma((heads,)),
                 dma((chunks,)),
                 dma((chunks,)),
-                dma((chunks,)),
             ],
             compiler_params=pltpu.CompilerParams(
-                collective_id=0, has_side_effects=True, vmem_limit_bytes=66 * 1024 * 1024 - 2 * 1024 * 1024 - 65536,
+                collective_id=0, has_side_effects=True, vmem_limit_bytes=57 * 1024 * 1024,
             ),
             name="attention_block",
         )(x_block, doc_block.reshape(1, rows), wqkv_block, wout_block)

time: 311 us -> 305 us (0.981)
  Pallas kernels: 307 us -> 303 us
    pallas_call x1, Pallas kernels: 307 us -> 303 us  [device_block(): pl.pallas_call(block_kernel, out_shape=pltpu.VMEM((rows // TP, cols * TP)...]
where the time goes in v2:
time: 305 us
  Pallas kernels  303 us (99%)
    pallas_call x1, Pallas kernels, device_block(): pl.pallas_call(block_kernel, out_shape=pltpu.VMEM((rows // TP, cols * TP)...  303 us

profile of v2, /device:TPU:0, one launch (start us, length us, event | category | flops | bytes accessed | tf_op | source)
XLA Modules:
  0.0 304.7 jit_solution(10798154672319567562)
XLA Ops:
  0.0 303.4 %attention_block.1 = bf16[256,4096]{1,0:T(8,128)(2,1)S(1)} custom-call(bf16[512,2048]{1,0:T(8,128)(2,1)} %x_ref.1, s32[1,512]{1,0:T(1,128)} %bitcast.1, bf16[1024,6144]{1,0:T(8,128)(2,1)} %wqkv_ref.1, bf16[1024,2048]{1,0:T(8,128)(2,1)} %wout_ref.1), custom_call_target="tpu_custom_call" | custom-call | tf_op jit(solution)/shard_map/attention_block/pallas_call | solution.py:292
  303.4 1.3 copy.6

commit v3 on v0

v3 whole, which is shorter than its diff:
```python
import jax
import jax.numpy as jnp
from jax import lax
from jax.experimental import pallas as pl
from jax.experimental.pallas import tpu as pltpu
from jax.sharding import PartitionSpec as P

HEAD_DIM = 128
SOFTMAX_SCALE = HEAD_DIM ** -0.5
TRIPLE = 3 * HEAD_DIM
SP = 4
TP = 2
WIDTH = 128
EARLY = 4
QUERIES = 256


def block_kernel(
    x_ref, doc_ref, wqkv_ref, wout_ref, y_ref,
    x_all, w_all, wo_all, o_all, qkv, doc_all,
    local_sem, x_send, x_recv, doc_send, doc_recv, w_send, w_recv, wo_send, wo_mate_recv,
    wo_recv, wo_pass_recv, o_send, o_recv, of_send, of_recv, y_send, y_recv,
):
    me = lax.axis_index("sp")
    col = lax.axis_index("tp")
    rows, half = x_ref.shape
    depth = wqkv_ref.shape[0]
    heads = w_all.shape[0]
    cols = wout_ref.shape[1]
    chunks = cols // WIDTH
    other_col = 1 - col
    chip = me // 2
    core = lax.rem(me, 2)
    mate = chip * 2 + 1 - core
    across = (1 - chip) * 2 + core
    diagonal = (1 - chip) * 2 + 1 - core
    peers = (mate, across, diagonal)
    to_mate, to_across, to_diagonal, to_col = {"sp": mate}, {"sp": across}, {"sp": diagonal}, {"tp": other_col}
    to_peers = (to_mate, to_across, to_diagonal)

    barrier = pltpu.get_barrier_semaphore()
    for where in (to_across, to_diagonal, to_col, to_mate):
        pl.semaphore_signal(barrier, inc=1, device_id=where, device_id_type=pl.DeviceIdType.MESH)
    pl.semaphore_wait(barrier, 4)

    def remote(src, dst, send, recv, where):
        return pltpu.make_async_remote_copy(
            src_ref=src, dst_ref=dst, send_sem=send, recv_sem=recv,
            device_id=where, device_id_type=pl.DeviceIdType.MESH,
        )

    def take(sem, ref):
        remote(ref, ref, sem, sem, to_mate).wait_recv()

    def local(src, dst, i):
        return pltpu.make_async_copy(src, dst, local_sem.at[i])

    def at(i, size):
        return pl.ds(pl.multiple_of(i * size, size), size)

    def x_slot(c, s):
        return x_all.at[c, at(s, rows), :]

    def x_pass(c, s, send, recv, where):
        remote(x_slot(c, s), x_slot(c, s), x_send.at[send], x_recv.at[recv], where).start()

    own_x = x_slot(col, me)
    remote(x_ref, own_x, x_send.at[0], x_recv.at[0], to_across).start()
    remote(x_ref, own_x, x_send.at[0], x_recv.at[1], to_col).start()
    remote(x_ref, own_x, x_send.at[0], x_recv.at[3], to_mate).start()
    local(x_ref, own_x, 0).start()
    for where in to_peers:
        remote(doc_ref, doc_all.at[me], doc_send, doc_recv, where).start()
    local(doc_ref, doc_all.at[me], 1).start()

    def w_cols(owner, h):
        return wqkv_ref.at[:, at(owner * heads + h, TRIPLE)]

    def w_slot(h, s):
        return w_all.at[h, at(s, depth), :]

    def w_go(i, h):
        remote(w_cols(peers[i], h), w_slot(h, me), w_send, w_recv.at[h], to_peers[i]).start()

    for h in range(heads):
        if h < heads - 1:
            w_go(1, h)
            w_go(2, h)
        w_go(0, h)
        local(w_cols(me, h), w_slot(h, me), 2).start()
    own_wo = wo_all.at[at(me, depth), :]
    local(wout_ref, own_wo, 3).start()

    take(x_recv.at[1], x_slot(other_col, me))
    x_pass(other_col, me, 1, 3, to_mate)
    take(x_recv.at[0], x_slot(col, across))
    x_pass(col, across, 1, 2, to_col)
    x_pass(col, across, 1, 3, to_mate)
    take(x_recv.at[2], x_slot(other_col, across))
    x_pass(other_col, across, 1, 3, to_mate)
    local(x_ref, own_x, 0).wait()
    local(doc_ref, doc_all.at[me], 1).wait()
    local(w_all.at[0], w_all.at[0], 2).wait()
    local(wout_ref, own_wo, 3).wait()
    take(doc_recv, doc_all.at[pl.ds(0, SP - 1)])
    take(x_recv.at[3], x_all.at[0])

    def wo_slot(s, j):
        return wo_all.at[at(s, depth), at(j, WIDTH)]

    def wo_go(j):
        remote(wout_ref.at[:, at(j, WIDTH)], wo_slot(me, j), wo_send.at[1], wo_recv.at[j], to_across).start()

    def wo_pass(j):
        remote(wo_slot(across, j), wo_slot(across, j), wo_send.at[2], wo_pass_recv.at[j], to_mate).start()

    def o_go(i, h):
        src = w_all.at[h, at(peers[i], rows), pl.ds(0, HEAD_DIM)]
        dst = o_all.at[col, me, :, at(h, HEAD_DIM)]
        remote(src, dst, o_send, o_recv.at[h], to_peers[i]).start()

    def o_pass(h):
        take(o_recv.at[h], w_all.at[0, pl.ds(0, rows), :])
        slot = o_all.at[col, :, :, at(h, HEAD_DIM)]
        remote(slot, slot, of_send, of_recv, to_col).start()

    def one_head(h, carry):
        take(w_recv.at[h], w_all.at[0, pl.ds(0, (SP - 1) * depth), :])

        def project(r, carry):
            tile = at(r, rows)
            total = jnp.dot(x_all[0, tile, :], w_all[h, :half, :], preferred_element_type=jnp.float32)
            total += jnp.dot(x_all[1, tile, :], w_all[h, half:, :], preferred_element_type=jnp.float32)
            qkv[tile, :] = total.astype(jnp.bfloat16)
            return carry

        lax.fori_loop(0, SP, project, 0)

        docs = jnp.concatenate([doc_all[s] for s in range(SP)], axis=1)
        per_block = rows // QUERIES

        def attend(r, carry):
            tile = at(r, QUERIES)
            scores = lax.dot_general(
                qkv[tile, :HEAD_DIM], qkv[:, HEAD_DIM:2 * HEAD_DIM], (((1,), (1,)), ((), ())),
                preferred_element_type=jnp.float32,
            ) * SOFTMAX_SCALE
            own = doc_all[r // per_block, :, at(lax.rem(r, per_block), QUERIES)]
            same = jnp.broadcast_to(own, (HEAD_DIM, QUERIES)).T[:, :1] == docs
            scores = jnp.where(same, scores, -jnp.inf)
            top = jnp.max(scores, axis=1, keepdims=True)
            weights = jnp.exp(scores - top)
            weights = weights * (1.0 / jnp.sum(weights, axis=1, keepdims=True))
            out = jnp.dot(weights.astype(jnp.bfloat16), qkv[:, 2 * HEAD_DIM:], preferred_element_type=jnp.float32)
            w_all[h, tile, :HEAD_DIM] = out.astype(jnp.bfloat16)
            return carry

        lax.fori_loop(0, SP * per_block, attend, 0)
        o_all[col, me, :, at(h, HEAD_DIM)] = w_all[h, at(me, rows), :HEAD_DIM]
        for i in (1, 2, 0):
            o_go(i, h)

        @pl.when(h == 0)
        def _():
            w_go(1, heads - 1)
            w_go(2, heads - 1)
            remote(wout_ref, own_wo, wo_send.at[0], wo_mate_recv, to_mate).start()

        @pl.when(h == heads - 2)
        def _():
            for j in range(EARLY):
                wo_go(j)
            o_pass(0)

        return carry

    lax.fori_loop(0, heads, one_head, 0)
    for j in range(EARLY, chunks):
        wo_go(j)
    for h in range(1, heads):
        o_pass(h)

    span = rows // 2
    keep = at(col, span)
    give = at(other_col, span)

    def y_go(j):
        src = w_all.at[heads - 1, at(j, span), pl.ds(HEAD_DIM, WIDTH)]
        remote(src, y_ref.at[:, at(col * chunks + j, WIDTH)], y_send, y_recv, to_col).start()

    def part(owner, piece, j):
        total = None
        for i in range(2):
            term = jnp.dot(
                o_all[owner // 2, lax.rem(owner, 2) * 2 + i, piece, :], wo_all[at(owner * 2 + i, depth // 2), at(j, WIDTH)],
                preferred_element_type=jnp.float32,
            )
            total = term if total is None else total + term
        return total

    take(wo_mate_recv, wo_all.at[pl.ds(0, depth), :])
    take(of_recv, o_all.at[0])

    take(x_send.at[0], x_all.at[0, pl.ds(0, 3 * rows), :])
    take(x_send.at[1], x_all.at[0])
    take(doc_send, doc_all.at[pl.ds(0, SP - 1)])
    take(w_send, w_all.at[pl.ds(0, SP - 1)])
    take(o_send, o_all.at[0, pl.ds(0, SP - 1)])
    take(of_send, o_all.at[0])
    take(wo_send.at[0], wo_all.at[pl.ds(0, depth), :])

    def finish(j, carry):
        given = part(me, give, j) + part(mate, give, j)
        kept = part(me, keep, j) + part(mate, keep, j)
        take(wo_recv.at[j], wo_slot(across, j))
        wo_pass(j)
        given += part(across, give, j)
        kept += part(across, keep, j)
        take(wo_pass_recv.at[j], wo_slot(diagonal, j))
        given += part(diagonal, give, j)
        w_all[heads - 1, at(j, span), HEAD_DIM:HEAD_DIM + WIDTH] = given.astype(jnp.bfloat16)
        y_go(j)
        kept += part(diagonal, keep, j)
        y_ref[:, at(col * chunks + j, WIDTH)] = kept.astype(jnp.bfloat16)
        return carry

    lax.fori_loop(0, chunks, finish, 0)
    take(wo_send.at[1], wo_all.at[pl.ds(0, depth), :])
    take(wo_send.at[2], wo_all.at[pl.ds(0, depth), :])
    take(y_send, y_ref.at[:, pl.ds(0, cols)])
    take(y_recv, y_ref.at[:, pl.ds(0, cols)])


def solution(mesh):
    def device_block(x_block, doc_block, wqkv_block, wout_block):
        rows, half = x_block.shape
        depth = wqkv_block.shape[0]
        heads = wqkv_block.shape[1] // (TRIPLE * SP)
        cols = wout_block.shape[1]
        chunks = cols // WIDTH
        bf16 = jnp.bfloat16
        dma = pltpu.SemaphoreType.DMA
        return pl.pallas_call(
            block_kernel,
            out_shape=pltpu.VMEM((rows // TP, cols * TP), bf16),
            in_specs=[pl.BlockSpec(memory_space=pl.ANY)] * 4,
            out_specs=pl.BlockSpec(memory_space=pltpu.VMEM),
            scratch_shapes=[
                pltpu.VMEM((TP, SP * rows, half), bf16),
                pltpu.VMEM((heads, SP * depth, TRIPLE), bf16),
                pltpu.VMEM((SP * depth, cols), bf16),
                pltpu.VMEM((TP, SP, rows, heads * HEAD_DIM), bf16),
                pltpu.VMEM((SP * rows, TRIPLE), bf16),
                pltpu.VMEM((SP, 1, rows), jnp.int32),
                dma((4,)),
                dma((2,)),
                dma((4,)),
                dma,
                dma,
                dma,
                dma((heads,)),
                dma((3,)),
                dma,
                dma((chunks,)),
                dma((chunks,)),
                dma,
                dma((heads,)),
                dma,
                dma,
                dma,
                dma,
            ],
            compiler_params=pltpu.CompilerParams(
                collective_id=0, has_side_effects=True, vmem_limit_bytes=57 * 1024 * 1024,
            ),
            name="attention_block",
        )(x_block, doc_block.reshape(1, rows), wqkv_block, wout_block)

    return jax.shard_map(
        device_block,
        mesh=mesh,
        in_specs=(P(("dp", "sp"), "tp"), P(("dp", "sp")), P("sp", "tp"), P("sp", "tp")),
        out_specs=P(("dp", "sp", "tp"), None),
        check_vma=False,
    )
```

time: 746 us -> 304 us (0.41)
  waiting for transfers between devices: 506 us -> 0 us
  Pallas kernels: 0 us -> 303 us
  matrix products: 102 us -> 0 us
  other arithmetic: 69.3 us -> 0 us
  blocking collectives: 34.4 us -> 0 us
  local copies, waits for them, and re-layouts: 20.9 us -> 1.32 us
  between operations: 13.2 us -> 0.01 us
    all_gather x5 -> x0, waiting for transfers between devices: 504 us -> none  [the longest x1 296 us: device_block(): wqkv_cols = lax.all_gather(wqkv_block, 'sp', axis=0, tiled=True)]
    pallas_call x0 -> x1, Pallas kernels: none -> 303 us  [device_block(): pl.pallas_call(block_kernel, out_shape=pltpu.VMEM((rows // TP, cols * TP)...]
    dot_general x4 -> x0, matrix products: 102 us -> none  [the longest x1 33.7 us: device_block(): jnp.dot(x_rows, wqkv_cols, preferred_element_type=jnp.float32)]
    sub x1 -> x0, other arithmetic: 68.7 us -> none  [device_block(): weights = jax.nn.softmax(scores, axis=-1).astype(jnp.bfloat16)]
    all_to_all x1 -> x0, blocking collectives: 27.4 us -> none  [device_block(): return lax.all_to_all(y_block, 'tp', 0, 1, tiled=True)]
    convert_element_type x1 -> x0, local copies, waits for them, and re-layouts: 8.64 us -> none  [device_block(): jnp.dot(x_rows, wqkv_cols, preferred_element_type=jnp.float32)]
  transfers between devices with their start and end apart: 5 -> 0, of which waited for: 4 -> 0; matrix products, arithmetic and copies ran while one was open for 17% -> 0% of each run, Pallas kernels for 0% -> 0%
where the time goes in v3:
time: 304 us
  Pallas kernels  303 us (100%)
    pallas_call x1, Pallas kernels, device_block(): pl.pallas_call(block_kernel, out_shape=pltpu.VMEM((rows // TP, cols * TP)...  303 us

profile of v3, /device:TPU:0, one launch (start us, length us, event | category | flops | bytes accessed | tf_op | source)
XLA Modules:
  0.0 304.0 jit_solution(17654883396088234138)
XLA Ops:
  0.0 302.7 %attention_block.1 = bf16[256,4096]{1,0:T(8,128)(2,1)S(1)} custom-call(bf16[512,2048]{1,0:T(8,128)(2,1)} %x_ref.1, s32[1,512]{1,0:T(1,128)} %bitcast.1, bf16[1024,6144]{1,0:T(8,128)(2,1)} %wqkv_ref.1, bf16[1024,2048]{1,0:T(8,128)(2,1)} %wout_ref.1), custom_call_target="tpu_custom_call" | custom-call | tf_op jit(solution)/shard_map/attention_block/pallas_call | solution.py:243
  302.7 1.3 copy.6

commit v4 on v3

--- a/solution.py
+++ b/solution.py
@@ -17,9 +17,10 @@
 
 def block_kernel(
     x_ref, doc_ref, wqkv_ref, wout_ref, y_ref,
-    x_all, w_all, wo_all, o_all, qkv, doc_all,
+    x_all, w_all, wo_all, o_all, o_mate, early_sums, qkv, doc_all,
     local_sem, x_send, x_recv, doc_send, doc_recv, w_send, w_recv, wo_send, wo_mate_recv,
     wo_recv, wo_pass_recv, o_send, o_recv, of_send, of_recv, y_send, y_recv,
+    last_send, last_recv, mate_send, mate_recv,
 ):
     me = lax.axis_index("sp")
     col = lax.axis_index("tp")
@@ -28,6 +29,7 @@
     heads = w_all.shape[0]
     cols = wout_ref.shape[1]
     chunks = cols // WIDTH
+    last = chunks - 1
     other_col = 1 - col
     chip = me // 2
     core = lax.rem(me, 2)
@@ -37,11 +39,12 @@
     peers = (mate, across, diagonal)
     to_mate, to_across, to_diagonal, to_col = {"sp": mate}, {"sp": across}, {"sp": diagonal}, {"tp": other_col}
     to_peers = (to_mate, to_across, to_diagonal)
+    to_col_mate = {"sp": mate, "tp": other_col}
 
     barrier = pltpu.get_barrier_semaphore()
-    for where in (to_across, to_diagonal, to_col, to_mate):
+    for where in (to_across, to_diagonal, to_col, to_col_mate, to_mate):
         pl.semaphore_signal(barrier, inc=1, device_id=where, device_id_type=pl.DeviceIdType.MESH)
-    pl.semaphore_wait(barrier, 4)
+    pl.semaphore_wait(barrier, 5)
 
     def remote(src, dst, send, recv, where):
         return pltpu.make_async_remote_copy(
@@ -175,8 +178,18 @@
         return carry
 
     lax.fori_loop(0, heads, one_head, 0)
-    for j in range(EARLY, chunks):
+    for j in range(EARLY, last):
         wo_go(j)
+    take(wo_mate_recv, wo_all.at[pl.ds(0, depth), :])
+
+    def last_go(i, src, owner):
+        remote(src, wo_slot(owner, last), last_send, last_recv.at[i], to_across).start()
+
+    @pl.when(core == 1)
+    def _():
+        last_go(0, wo_slot(mate, last), mate)
+        last_go(1, wout_ref.at[:, at(last, WIDTH)], me)
+
     for h in range(1, heads):
         o_pass(h)
 
@@ -184,22 +197,30 @@
     keep = at(col, span)
     give = at(other_col, span)
 
+    def stage(j, k):
+        return w_all.at[heads - 1, at(j, span), pl.ds(k * HEAD_DIM, WIDTH)]
+
+    def y_slot(j):
+        return y_ref.at[:, at(col * chunks + j, WIDTH)]
+
     def y_go(j):
-        src = w_all.at[heads - 1, at(j, span), pl.ds(HEAD_DIM, WIDTH)]
-        remote(src, y_ref.at[:, at(col * chunks + j, WIDTH)], y_send, y_recv, to_col).start()
-
-    def part(owner, piece, j):
+        remote(stage(j, 1), y_slot(j), y_send, y_recv, to_col).start()
+
+    def part(source, owner, piece, j):
         total = None
         for i in range(2):
             term = jnp.dot(
-                o_all[owner // 2, lax.rem(owner, 2) * 2 + i, piece, :], wo_all[at(owner * 2 + i, depth // 2), at(j, WIDTH)],
+                source[owner // 2, lax.rem(owner, 2) * 2 + i, piece, :], wo_all[at(owner * 2 + i, depth // 2), at(j, WIDTH)],
                 preferred_element_type=jnp.float32,
             )
             total = term if total is None else total + term
         return total
 
-    take(wo_mate_recv, wo_all.at[pl.ds(0, depth), :])
     take(of_recv, o_all.at[0])
+
+    @pl.when(core == 0)
+    def _():
+        remote(o_all, o_mate, mate_send.at[0], mate_recv.at[0], to_mate).start()
 
     take(x_send.at[0], x_all.at[0, pl.ds(0, 3 * rows), :])
     take(x_send.at[1], x_all.at[0])
@@ -209,25 +230,64 @@
     take(of_send, o_all.at[0])
     take(wo_send.at[0], wo_all.at[pl.ds(0, depth), :])
 
+    blocks = ((o_mate, give), (o_all, give), (o_mate, keep), (o_all, keep))
+
     def finish(j, carry):
-        given = part(me, give, j) + part(mate, give, j)
-        kept = part(me, keep, j) + part(mate, keep, j)
+        @pl.when((j == last - 3) & (core == 1))
+        def _():
+            take(mate_recv.at[0], o_mate)
+            for i, (source, piece) in enumerate(blocks):
+                early_sums[i] = part(source, me, piece, last) + part(source, mate, piece, last)
+
+        given = part(o_all, me, give, j) + part(o_all, mate, give, j)
+        kept = part(o_all, me, keep, j) + part(o_all, mate, keep, j)
         take(wo_recv.at[j], wo_slot(across, j))
         wo_pass(j)
-        given += part(across, give, j)
-        kept += part(across, keep, j)
+        given += part(o_all, across, give, j)
+        kept += part(o_all, across, keep, j)
         take(wo_pass_recv.at[j], wo_slot(diagonal, j))
-        given += part(diagonal, give, j)
-        w_all[heads - 1, at(j, span), HEAD_DIM:HEAD_DIM + WIDTH] = given.astype(jnp.bfloat16)
+        given += part(o_all, diagonal, give, j)
+        stage(j, 1)[...] = given.astype(jnp.bfloat16)
         y_go(j)
-        kept += part(diagonal, keep, j)
-        y_ref[:, at(col * chunks + j, WIDTH)] = kept.astype(jnp.bfloat16)
+        kept += part(o_all, diagonal, keep, j)
+        y_slot(j)[...] = kept.astype(jnp.bfloat16)
         return carry
 
-    lax.fori_loop(0, chunks, finish, 0)
-    take(wo_send.at[1], wo_all.at[pl.ds(0, depth), :])
-    take(wo_send.at[2], wo_all.at[pl.ds(0, depth), :])
-    take(y_send, y_ref.at[:, pl.ds(0, cols)])
+    lax.fori_loop(0, last, finish, 0)
+    most = pl.ds(0, last * WIDTH)
+
+    @pl.when(core == 1)
+    def _():
+        take(last_recv.at[0], wo_slot(diagonal, last))
+        totals = [early_sums[i] + part(source, diagonal, piece, last) for i, (source, piece) in enumerate(blocks)]
+        take(last_recv.at[1], wo_slot(across, last))
+
+        def whole(i):
+            source, piece = blocks[i]
+            return (totals[i] + part(source, across, piece, last)).astype(jnp.bfloat16)
+
+        stage(0, 2)[...] = whole(0)
+        to_col_mate_copy = remote(stage(0, 2), y_slot(last), mate_send.at[1], y_recv, to_col_mate)
+        to_col_mate_copy.start()
+        stage(last, 1)[...] = whole(1)
+        y_go(last)
+        stage(1, 2)[...] = whole(2)
+        kept_copy = remote(stage(1, 2), y_slot(last), mate_send.at[2], mate_recv.at[1], to_mate)
+        kept_copy.start()
+        y_slot(last)[...] = whole(3)
+        take(last_send, wo_all.at[pl.ds(0, depth), pl.ds(0, 2 * WIDTH)])
+        take(y_send, y_ref.at[:, pl.ds(0, cols)])
+        to_col_mate_copy.wait_send()
+        kept_copy.wait_send()
+
+    @pl.when(core == 0)
+    def _():
+        take(mate_send.at[0], o_all)
+        take(y_send, y_ref.at[:, most])
+        take(mate_recv.at[1], y_slot(last))
+
+    take(wo_send.at[1], wo_all.at[pl.ds(0, depth), most])
+    take(wo_send.at[2], wo_all.at[pl.ds(0, depth), most])
     take(y_recv, y_ref.at[:, pl.ds(0, cols)])
 
 
@@ -250,6 +310,8 @@
                 pltpu.VMEM((heads, SP * depth, TRIPLE), bf16),
                 pltpu.VMEM((SP * depth, cols), bf16),
                 pltpu.VMEM((TP, SP, rows, heads * HEAD_DIM), bf16),
+                pltpu.VMEM((TP, SP, rows, heads * HEAD_DIM), bf16),
+                pltpu.VMEM((4, rows // 2, WIDTH), jnp.float32),
                 pltpu.VMEM((SP * rows, TRIPLE), bf16),
                 pltpu.VMEM((SP, 1, rows), jnp.int32),
                 dma((4,)),
@@ -261,17 +323,21 @@
                 dma((heads,)),
                 dma((3,)),
                 dma,
-                dma((chunks,)),
-                dma((chunks,)),
+                dma((chunks - 1,)),
+                dma((chunks - 1,)),
                 dma,
                 dma((heads,)),
                 dma,
                 dma,
                 dma,
                 dma,
+                dma,
+                dma((2,)),
+                dma((3,)),
+                dma((2,)),
             ],
             compiler_params=pltpu.CompilerParams(
-                collective_id=0, has_side_effects=True, vmem_limit_bytes=57 * 1024 * 1024,
+                collective_id=0, has_side_effects=True, vmem_limit_bytes=60 * 1024 * 1024,
             ),
             name="attention_block",
         )(x_block, doc_block.reshape(1, rows), wqkv_block, wout_block)

time: 304 us -> 302 us (level)
  no operation moved by 1% of the time
where the time goes in v4:
time: 302 us
  Pallas kernels  301 us (100%)
    pallas_call x1, Pallas kernels, device_block(): pl.pallas_call(block_kernel, out_shape=pltpu.VMEM((rows // TP, cols * TP)...  301 us

profile of v4, /device:TPU:0, one launch (start us, length us, event | category | flops | bytes accessed | tf_op | source)
XLA Modules:
  0.0 302.2 jit_solution(6227387187814359026)
XLA Ops:
  0.0 300.9 %attention_block.1 = bf16[256,4096]{1,0:T(8,128)(2,1)S(1)} custom-call(bf16[512,2048]{1,0:T(8,128)(2,1)} %x_ref.1, s32[1,512]{1,0:T(1,128)} %bitcast.1, bf16[1024,6144]{1,0:T(8,128)(2,1)} %wqkv_ref.1, bf16[1024,2048]{1,0:T(8,128)(2,1)} %wout_ref.1), custom_call_target="tpu_custom_call" | custom-call | tf_op jit(solution)/shard_map/attention_block/pallas_call | solution.py:303
  300.9 1.3 copy.6

commit v5 on v4

--- a/solution.py
+++ b/solution.py
@@ -11,16 +11,16 @@
 SP = 4
 TP = 2
 WIDTH = 128
-EARLY = 4
+PIECES = (4, 4, 1, 1, 1, 1, 1, 1, 1)
+ALONE = 8
 QUERIES = 256
 
 
 def block_kernel(
     x_ref, doc_ref, wqkv_ref, wout_ref, y_ref,
     x_all, w_all, wo_all, o_all, o_mate, early_sums, qkv, doc_all,
-    local_sem, x_send, x_recv, doc_send, doc_recv, w_send, w_recv, wo_send, wo_mate_recv,
-    wo_recv, wo_pass_recv, o_send, o_recv, of_send, of_recv, y_send, y_recv,
-    last_send, last_recv, mate_send, mate_recv,
+    local_sem, x_send, x_recv, doc_send, doc_recv, w_send, w_recv, late_send, wo_mate_recv,
+    wo_recv, wo_pass_recv, o_recv, of_recv, y_recv, last_recv, mate_send, mate_recv,
 ):
     me = lax.axis_index("sp")
     col = lax.axis_index("tp")
@@ -64,13 +64,13 @@
     def x_slot(c, s):
         return x_all.at[c, at(s, rows), :]
 
-    def x_pass(c, s, send, recv, where):
-        remote(x_slot(c, s), x_slot(c, s), x_send.at[send], x_recv.at[recv], where).start()
+    def x_pass(c, s, recv, where):
+        remote(x_slot(c, s), x_slot(c, s), x_send, x_recv.at[recv], where).start()
 
     own_x = x_slot(col, me)
-    remote(x_ref, own_x, x_send.at[0], x_recv.at[0], to_across).start()
-    remote(x_ref, own_x, x_send.at[0], x_recv.at[1], to_col).start()
-    remote(x_ref, own_x, x_send.at[0], x_recv.at[3], to_mate).start()
+    remote(x_ref, own_x, x_send, x_recv.at[0], to_across).start()
+    remote(x_ref, own_x, x_send, x_recv.at[1], to_col).start()
+    remote(x_ref, own_x, x_send, x_recv.at[3], to_mate).start()
     local(x_ref, own_x, 0).start()
     for where in to_peers:
         remote(doc_ref, doc_all.at[me], doc_send, doc_recv, where).start()
@@ -90,42 +90,44 @@
             w_go(1, h)
             w_go(2, h)
         w_go(0, h)
-        local(w_cols(me, h), w_slot(h, me), 2).start()
+        local(w_cols(me, h), w_slot(h, me), 0).start()
     own_wo = wo_all.at[at(me, depth), :]
-    local(wout_ref, own_wo, 3).start()
+    local(wout_ref, own_wo, 0).start()
 
     take(x_recv.at[1], x_slot(other_col, me))
-    x_pass(other_col, me, 1, 3, to_mate)
+    x_pass(other_col, me, 3, to_mate)
     take(x_recv.at[0], x_slot(col, across))
-    x_pass(col, across, 1, 2, to_col)
-    x_pass(col, across, 1, 3, to_mate)
+    x_pass(col, across, 2, to_col)
+    x_pass(col, across, 3, to_mate)
     take(x_recv.at[2], x_slot(other_col, across))
-    x_pass(other_col, across, 1, 3, to_mate)
-    local(x_ref, own_x, 0).wait()
+    x_pass(other_col, across, 3, to_mate)
+    mine = wo_all.at[pl.ds(0, (rows * half + heads * depth * TRIPLE + depth * cols) // cols), :]
+    local(mine, mine, 0).wait()
     local(doc_ref, doc_all.at[me], 1).wait()
-    local(w_all.at[0], w_all.at[0], 2).wait()
-    local(wout_ref, own_wo, 3).wait()
     take(doc_recv, doc_all.at[pl.ds(0, SP - 1)])
     take(x_recv.at[3], x_all.at[0])
 
-    def wo_slot(s, j):
-        return wo_all.at[at(s, depth), at(j, WIDTH)]
-
-    def wo_go(j):
-        remote(wout_ref.at[:, at(j, WIDTH)], wo_slot(me, j), wo_send.at[1], wo_recv.at[j], to_across).start()
-
-    def wo_pass(j):
-        remote(wo_slot(across, j), wo_slot(across, j), wo_send.at[2], wo_pass_recv.at[j], to_mate).start()
+    def wo_slot(s, j, count=1):
+        return wo_all.at[at(s, depth), pl.ds(pl.multiple_of(j * WIDTH, WIDTH), count * WIDTH)]
+
+    def wo_go(p):
+        j, count = sum(PIECES[:p]), PIECES[p]
+        src = wout_ref.at[:, pl.ds(j * WIDTH, count * WIDTH)]
+        remote(src, wo_slot(me, j, count), late_send, wo_recv.at[p], to_across).start()
+
+    def wo_pass(p, j, count):
+        take(wo_recv.at[p], wo_slot(across, j, count))
+        remote(wo_slot(across, j, count), wo_slot(across, j, count), late_send, wo_pass_recv.at[p], to_mate).start()
 
     def o_go(i, h):
         src = w_all.at[h, at(peers[i], rows), pl.ds(0, HEAD_DIM)]
         dst = o_all.at[col, me, :, at(h, HEAD_DIM)]
-        remote(src, dst, o_send, o_recv.at[h], to_peers[i]).start()
+        remote(src, dst, late_send, o_recv.at[h], to_peers[i]).start()
 
     def o_pass(h):
         take(o_recv.at[h], w_all.at[0, pl.ds(0, rows), :])
         slot = o_all.at[col, :, :, at(h, HEAD_DIM)]
-        remote(slot, slot, of_send, of_recv, to_col).start()
+        remote(slot, slot, late_send, of_recv, to_col).start()
 
     def one_head(h, carry):
         take(w_recv.at[h], w_all.at[0, pl.ds(0, (SP - 1) * depth), :])
@@ -167,28 +169,32 @@
         def _():
             w_go(1, heads - 1)
             w_go(2, heads - 1)
-            remote(wout_ref, own_wo, wo_send.at[0], wo_mate_recv, to_mate).start()
+            remote(wout_ref, own_wo, late_send, wo_mate_recv, to_mate).start()
 
         @pl.when(h == heads - 2)
         def _():
-            for j in range(EARLY):
-                wo_go(j)
+            wo_go(0)
             o_pass(0)
 
         return carry
 
     lax.fori_loop(0, heads, one_head, 0)
-    for j in range(EARLY, last):
-        wo_go(j)
+    for p in range(1, len(PIECES)):
+        wo_go(p)
+
     take(wo_mate_recv, wo_all.at[pl.ds(0, depth), :])
 
-    def last_go(i, src, owner):
-        remote(src, wo_slot(owner, last), last_send, last_recv.at[i], to_across).start()
+    def last_slot(s, i, count=1):
+        return wo_all.at[pl.ds(pl.multiple_of(s * depth + i * (depth // 2), depth // 2), count * (depth // 2)), at(last, WIDTH)]
+
+    def last_go(k, src, owner, i, count=1):
+        remote(src, last_slot(owner, i, count), mate_send, last_recv.at[k], to_across).start()
 
     @pl.when(core == 1)
     def _():
-        last_go(0, wo_slot(mate, last), mate)
-        last_go(1, wout_ref.at[:, at(last, WIDTH)], me)
+        last_go(0, last_slot(mate, 0, 2), mate, 0, 2)
+        for i in range(2):
+            last_go(1 + i, wout_ref.at[pl.ds(i * (depth // 2), depth // 2), at(last, WIDTH)], me, i)
 
     for h in range(1, heads):
         o_pass(h)
@@ -203,12 +209,12 @@
     def y_slot(j):
         return y_ref.at[:, at(col * chunks + j, WIDTH)]
 
-    def y_go(j):
-        remote(stage(j, 1), y_slot(j), y_send, y_recv, to_col).start()
-
-    def part(source, owner, piece, j):
+    def y_go(j, send=None):
+        remote(stage(j, 1), y_slot(j), late_send if send is None else send, y_recv, to_col).start()
+
+    def part(source, owner, piece, j, halves=(0, 1)):
         total = None
-        for i in range(2):
+        for i in halves:
             term = jnp.dot(
                 source[owner // 2, lax.rem(owner, 2) * 2 + i, piece, :], wo_all[at(owner * 2 + i, depth // 2), at(j, WIDTH)],
                 preferred_element_type=jnp.float32,
@@ -220,15 +226,10 @@
 
     @pl.when(core == 0)
     def _():
-        remote(o_all, o_mate, mate_send.at[0], mate_recv.at[0], to_mate).start()
-
-    take(x_send.at[0], x_all.at[0, pl.ds(0, 3 * rows), :])
-    take(x_send.at[1], x_all.at[0])
+        remote(o_all, o_mate, mate_send, mate_recv.at[0], to_mate).start()
+
     take(doc_send, doc_all.at[pl.ds(0, SP - 1)])
     take(w_send, w_all.at[pl.ds(0, SP - 1)])
-    take(o_send, o_all.at[0, pl.ds(0, SP - 1)])
-    take(of_send, o_all.at[0])
-    take(wo_send.at[0], wo_all.at[pl.ds(0, depth), :])
 
     blocks = ((o_mate, give), (o_all, give), (o_mate, keep), (o_all, keep))
 
@@ -241,11 +242,18 @@
 
         given = part(o_all, me, give, j) + part(o_all, mate, give, j)
         kept = part(o_all, me, keep, j) + part(o_all, mate, keep, j)
-        take(wo_recv.at[j], wo_slot(across, j))
-        wo_pass(j)
+
+        @pl.when(j >= ALONE)
+        def _():
+            wo_pass(j - shift, j, 1)
+
         given += part(o_all, across, give, j)
         kept += part(o_all, across, keep, j)
-        take(wo_pass_recv.at[j], wo_slot(diagonal, j))
+
+        @pl.when(j >= ALONE)
+        def _():
+            take(wo_pass_recv.at[j - shift], wo_slot(diagonal, j))
+
         given += part(o_all, diagonal, give, j)
         stage(j, 1)[...] = given.astype(jnp.bfloat16)
         y_go(j)
@@ -253,41 +261,46 @@
         y_slot(j)[...] = kept.astype(jnp.bfloat16)
         return carry
 
+    wide = len(PIECES) - (last - ALONE)
+    shift = ALONE - wide
+    for p in range(wide):
+        wo_pass(p, sum(PIECES[:p]), PIECES[p])
+    for p in range(wide):
+        take(wo_pass_recv.at[p], wo_slot(diagonal, sum(PIECES[:p]), PIECES[p]))
     lax.fori_loop(0, last, finish, 0)
     most = pl.ds(0, last * WIDTH)
 
     @pl.when(core == 1)
     def _():
-        take(last_recv.at[0], wo_slot(diagonal, last))
+        take(last_recv.at[0], last_slot(diagonal, 0, 2))
         totals = [early_sums[i] + part(source, diagonal, piece, last) for i, (source, piece) in enumerate(blocks)]
-        take(last_recv.at[1], wo_slot(across, last))
+        take(last_recv.at[1], last_slot(across, 0))
+        totals = [total + part(source, across, piece, last, (0,)) for total, (source, piece) in zip(totals, blocks)]
+        take(last_recv.at[2], last_slot(across, 1))
 
         def whole(i):
             source, piece = blocks[i]
-            return (totals[i] + part(source, across, piece, last)).astype(jnp.bfloat16)
+            return (totals[i] + part(source, across, piece, last, (1,))).astype(jnp.bfloat16)
 
         stage(0, 2)[...] = whole(0)
-        to_col_mate_copy = remote(stage(0, 2), y_slot(last), mate_send.at[1], y_recv, to_col_mate)
+        to_col_mate_copy = remote(stage(0, 2), y_slot(last), mate_send, y_recv, to_col_mate)
         to_col_mate_copy.start()
         stage(last, 1)[...] = whole(1)
-        y_go(last)
+        y_go(last, mate_send)
         stage(1, 2)[...] = whole(2)
-        kept_copy = remote(stage(1, 2), y_slot(last), mate_send.at[2], mate_recv.at[1], to_mate)
+        kept_copy = remote(stage(1, 2), y_slot(last), mate_send, mate_recv.at[1], to_mate)
         kept_copy.start()
         y_slot(last)[...] = whole(3)
-        take(last_send, wo_all.at[pl.ds(0, depth), pl.ds(0, 2 * WIDTH)])
-        take(y_send, y_ref.at[:, pl.ds(0, cols)])
-        to_col_mate_copy.wait_send()
-        kept_copy.wait_send()
+        take(mate_send, wo_all.at[pl.ds(0, (2 * depth + 3 * span) * WIDTH // cols), :])
 
     @pl.when(core == 0)
     def _():
-        take(mate_send.at[0], o_all)
-        take(y_send, y_ref.at[:, most])
+        take(mate_send, wo_all.at[pl.ds(0, TP * rows), :])
         take(mate_recv.at[1], y_slot(last))
 
-    take(wo_send.at[1], wo_all.at[pl.ds(0, depth), most])
-    take(wo_send.at[2], wo_all.at[pl.ds(0, depth), most])
+    take(x_send, wo_all.at[pl.ds(0, 7 * rows), :])
+    late = 12 * rows * HEAD_DIM + 4 * rows * cols // SP + depth * cols + 2 * depth * last * WIDTH + span * last * WIDTH
+    take(late_send, wo_all.at[pl.ds(0, late // cols), :])
     take(y_recv, y_ref.at[:, pl.ds(0, cols)])
 
 
@@ -297,7 +310,6 @@
         depth = wqkv_block.shape[0]
         heads = wqkv_block.shape[1] // (TRIPLE * SP)
         cols = wout_block.shape[1]
-        chunks = cols // WIDTH
         bf16 = jnp.bfloat16
         dma = pltpu.SemaphoreType.DMA
         return pl.pallas_call(
@@ -314,26 +326,22 @@
                 pltpu.VMEM((4, rows // 2, WIDTH), jnp.float32),
                 pltpu.VMEM((SP * rows, TRIPLE), bf16),
                 pltpu.VMEM((SP, 1, rows), jnp.int32),
+                dma((2,)),
+                dma,
                 dma((4,)),
-                dma((2,)),
-                dma((4,)),
                 dma,
                 dma,
                 dma,
                 dma((heads,)),
+                dma,
+                dma,
+                dma((len(PIECES),)),
+                dma((len(PIECES),)),
+                dma((heads,)),
+                dma,
+                dma,
                 dma((3,)),
                 dma,
-                dma((chunks - 1,)),
-                dma((chunks - 1,)),
-                dma,
-                dma((heads,)),
-                dma,
-                dma,
-                dma,
-                dma,
-                dma,
-                dma((2,)),
-                dma((3,)),
                 dma((2,)),
             ],
             compiler_params=pltpu.CompilerParams(

time: 302 us -> 302 us (level)
  no operation moved by 1% of the time
where the time goes in v5:
time: 302 us
  Pallas kernels  301 us (100%)
    pallas_call x1, Pallas kernels, device_block(): pl.pallas_call(block_kernel, out_shape=pltpu.VMEM((rows // TP, cols * TP)...  301 us

profile of v5, /device:TPU:0, one launch (start us, length us, event | category | flops | bytes accessed | tf_op | source)
XLA Modules:
  0.0 302.0 jit_solution(4327705659527958344)
XLA Ops:
  0.0 300.7 %attention_block.1 = bf16[256,4096]{1,0:T(8,128)(2,1)S(1)} custom-call(bf16[512,2048]{1,0:T(8,128)(2,1)} %x_ref.1, s32[1,512]{1,0:T(1,128)} %bitcast.1, bf16[1024,6144]{1,0:T(8,128)(2,1)} %wqkv_ref.1, bf16[1024,2048]{1,0:T(8,128)(2,1)} %wout_ref.1), custom_call_target="tpu_custom_call" | custom-call | tf_op jit(solution)/shard_map/attention_block/pallas_call | solution.py:315
  300.7 1.3 copy.6
